TPU v7x, 32 devices: a whole 2x2x4 slice. The times are simulated.
32 devices in a mesh: gx: 4 (over y, x), gy: 8 (over z, core).
Axes of the slice: x: 2, y: 2, z: 4, core: 2. Of those that a mesh axis runs over, the one named last changes fastest.
Arguments:
- replay_deter: float32 [8192, 2048], P(('gx', 'gy')), may hold values from -1 to 1
- replay_stoch: int32 [8192, 32], P(('gx', 'gy')), may hold values from 0 to 31
- send_rows: int32 [1024, 8], P(('gx', 'gy')), may hold values from 0 to 255
- send_counts: int32 [32, 32], P(('gx', 'gy')), may hold values from 0 to 8, as said below
- actions: int32 [8192, 4], P(('gx', 'gy')), may hold values from 0 to 17
- samples: int32 [8192, 4, 32], P(('gx', 'gy')), may hold values from 0 to 31
- w_stoch: bfloat16 [1024, 6144], P('gy'), may hold values from -1 to 1
- w_deter: bfloat16 [4, 512, 1536], P(None, 'gy'), may hold values from -0.25 to 0.25
- act_table: bfloat16 [18, 6144], replicated, may hold values from -3 to 3
- w_prior: bfloat16 [2048, 1024], P('gy'), may hold values from -0.037353516 to 0.037353516
Outputs:
- imagined: bfloat16 [8192, 4, 2048], P(('gx', 'gy'))
- log_prob: float32 [8192, 4, 32], P(('gx', 'gy'))
Inputs may be any that keep to these rules, and one draw needn't show every extreme that they name: `send_rows`: entries past a destination's count are unused. `send_counts`: each source's counts sum to exactly 128; every source sends 8 rows to some owner, and some owner receives 8 rows from every source.
All inputs are finite; a program needn't handle non-finite values.
Results may differ from a plain program's by a relative error of at most 0.0022.
Values may be sent and summed in bfloat16 or wider, within the bound.
No kernel may reach another device: no remote copies, remote signals or barrier semaphores. Data moves between devices by JAX's collectives and lax.ppermute only.
A program may use at most 128 MiB of HBM per device.

v0:
```python
import jax
import jax.numpy as jnp
from jax import lax
from jax.sharding import PartitionSpec as P

GROUPS = 32
CLASSES = 32
STEPS = 4


def gate_inputs(stoch, action, actions_count):
    rows = stoch.shape[0]
    onehot = (
        (stoch[:, :, None] == jnp.arange(CLASSES, dtype=jnp.int32)[None, None, :])
        .reshape(rows, GROUPS * CLASSES)
        .astype(jnp.bfloat16)
    )
    act_hot = (action[:, None] == jnp.arange(actions_count, dtype=jnp.int32)[None, :]).astype(
        jnp.bfloat16
    )
    return (onehot, act_hot)


def imagine(start, first, acts, samps, stoch_full, deter_full, act_table):
    blocks = deter_full.shape[0]
    width = deter_full.shape[1]
    pieces = [start[:, b * width : (b + 1) * width] for b in range(blocks)]
    stoch = first
    states = []
    for step in range(STEPS):
        onehot, act_hot = gate_inputs(stoch, acts[:, step], act_table.shape[0])
        input_term = jnp.dot(onehot, stoch_full, preferred_element_type=jnp.float32) + jnp.dot(
            act_hot, act_table, preferred_element_type=jnp.float32
        )
        fresh = []
        for b in range(blocks):
            before = pieces[b]
            gates = input_term[:, 3 * width * b : 3 * width * (b + 1)] + jnp.dot(
                before.astype(jnp.bfloat16), deter_full[b], preferred_element_type=jnp.float32
            )
            reset = jax.nn.sigmoid(gates[:, :width])
            cand = jnp.tanh(reset * gates[:, width : 2 * width])
            update = jax.nn.sigmoid(gates[:, 2 * width :] - 1.0)
            fresh.append(update * cand + (1.0 - update) * before)
        pieces = fresh
        states.append(jnp.concatenate(pieces, 1).astype(jnp.bfloat16))
        stoch = samps[:, step]
    return jnp.stack(states, 1)


def on_device(
    replay_deter,
    replay_stoch,
    send_rows,
    send_counts,
    actions,
    samples,
    w_stoch,
    w_deter,
    act_table,
    w_prior,
):
    peers, cap = send_rows.shape
    slots = peers * cap
    deter = replay_deter.shape[1]
    stoch_full = lax.all_gather(w_stoch, "gy", axis=0, tiled=True)
    deter_full = lax.all_gather(w_deter, "gy", axis=1, tiled=True)
    outgoing = (jnp.arange(cap, dtype=jnp.int32)[None, :] < send_counts[0][:, None]).astype(
        jnp.int32
    )
    start = replay_deter[send_rows]
    first = replay_stoch[send_rows]
    start, first, live = (
        lax.all_to_all(start, ("gx", "gy"), split_axis=0, concat_axis=0, tiled=True),
        lax.all_to_all(first, ("gx", "gy"), split_axis=0, concat_axis=0, tiled=True),
        lax.all_to_all(outgoing, ("gx", "gy"), split_axis=0, concat_axis=0, tiled=True),
    )
    live = live.reshape(slots)
    states = imagine(
        start.reshape(slots, deter),
        first.reshape(slots, GROUPS),
        actions,
        samples,
        stoch_full,
        deter_full,
        act_table,
    )
    states = jnp.where(live[:, None, None] > 0, states, jnp.zeros_like(states))
    prior_full = lax.all_gather(w_prior, "gy", axis=0, tiled=True)
    logits = jnp.dot(
        states.reshape(slots * STEPS, deter), prior_full, preferred_element_type=jnp.float32
    )
    logits = logits.reshape(slots, STEPS, GROUPS, CLASSES)
    totals = jnp.log(jnp.sum(jnp.exp(logits), -1))
    hits = samples[..., None] == jnp.arange(CLASSES, dtype=jnp.int32)
    picked = jnp.sum(jnp.where(hits, logits, jnp.zeros_like(logits)), -1)
    log_prob = jnp.where(live[:, None, None] > 0, picked - totals, jnp.zeros_like(totals))
    return (states, log_prob)


def solution(mesh):
    in_specs = (
        P(("gx", "gy"), None),
        P(("gx", "gy"), None),
        P(("gx", "gy"), None),
        P(("gx", "gy"), None),
        P(("gx", "gy"), None),
        P(("gx", "gy"), None, None),
        P("gy", None),
        P(None, "gy", None),
        P(),
        P("gy", None),
    )
    out_specs = (P(("gx", "gy"), None, None), P(("gx", "gy"), None, None))
    return jax.shard_map(
        on_device, mesh=mesh, in_specs=in_specs, out_specs=out_specs, check_vma=False
    )
```

profile of v0, /device:TPU:0, one launch (start us, length us, event | category | flops | bytes accessed | tf_op | source)
XLA Modules:
  0.0 338.7 jit_solution(16087413320578995944)
XLA Ops:
  7.2 0.7 all-gather.8.cloned.1.call-update
  8.0 0.7 all-gather.4.cloned.1.call-update
  8.7 0.7 all-gather.6.cloned.1.call-update
  9.4 1.4 compare_convert_fusion
  10.8 7.3 %all-to-all-start = ((s32[32,1,8]{2,1,0:T(1,128)}), s32[32,1,8]{2,1,0:T(1,128)S(1)}, u32[]{:S(2)}, u32[]{:S(2)}) async-start(s32[32,1,8]{2,1,0:T(1,128)} %compare_convert_fusion), calls=%async_computation | async-start | bytes 32768 | tf_op jit(solution)/shard_map/all_to_all | solution.py:76
  18.1 0.7 compare_select_fusion
  19.0 0.9 copy.24
  19.8 0.7 gather_fusion
  20.6 0.7 reshape.433
  21.3 3.9 %all-to-all-done = s32[32,1,8]{2,1,0:T(1,128)S(1)} async-done(((s32[32,1,8]{2,1,0:T(1,128)}), s32[32,1,8]{2,1,0:T(1,128)S(1)}, u32[]{:S(2)}, u32[]{:S(2)}) %all-to-all-start) | async-done | bytes 1056 | tf_op jit(solution)/shard_map/all_to_all | solution.py:76
  25.2 2.6 all-to-all-start.1
  27.8 2.7 gather_fusion.1
  30.5 5.0 %all-to-all-done.1 = s32[32,1,256]{2,1,0:T(1,128)S(1)} async-done(((s32[32,1,256]{2,1,0:T(1,128)}), s32[32,1,256]{2,1,0:T(1,128)S(1)}, u32[]{:S(2)}, u32[]{:S(2)}) %all-to-all-start.1) | async-done | bytes 32800 | tf_op jit(solution)/shard_map/all_to_all | solution.py:75
  35.4 2.7 all-to-all-start.2
  39.0 0.7 reduce.2
  39.8 1.5 bitcast_compare_fusion
  41.3 41.9 %all-gather.8.cloned.1.call-done = bf16[2048,1024]{1,0:T(8,128)(2,1)} async-done(((bf16[256,1024]{1,0:T(8,128)(2,1)}), bf16[2048,1024]{1,0:T(8,128)(2,1)}) %all-gather.8.cloned.1.call-update) | async-done | bytes 4194320 | tf_op jit(solution)/shard_map/all_gather | solution.py:89
  83.2 6.5 %copy.26 = bf16[1024,2048]{1,0:T(8,128)(2,1)} copy(bf16[1024,2048]{0,1:T(8,128)(2,1)} %bitcast.116) | data formatting | bytes 8388608 | tf_op jit(solution)/shard_map/dot_general | solution.py:90
  89.7 116.9 %all-gather.4.cloned.1.call-done = bf16[1024,6144]{1,0:T(8,128)(2,1)} async-done(((bf16[128,6144]{1,0:T(8,128)(2,1)}), bf16[1024,6144]{1,0:T(8,128)(2,1)}) %all-gather.4.cloned.1.call-update) | async-done | bytes 12582928 | tf_op jit(solution)/shard_map/all_gather | solution.py:66
  206.6 7.0 %fusion.199 = f32[256,6144]{1,0:T(8,128)S(1)} fusion(pred[256,1024]{0,1:T(32,128)(4,1)S(1)} %get-tuple-element.50, bf16[1024,6144]{1,0:T(8,128)(2,1)} %all-gather.4.cloned.1.call-done), kind=kOutput, calls=%fused_computation.297 | convolution fusion | flops 3221225472 | bytes 19136512 | tf_op jit(solution)/shard_map/dot_general | solution.py:32
  213.6 3.7 %convolution_add_fusion.3 = f32[256,6144]{1,0:T(8,128)} fusion(f32[256,6144]{1,0:T(8,128)S(1)} %fusion.199, bf16[18,6144]{1,0:T(8,128)(2,1)S(1)} %copy-done.3, s32[256]{0:T(256)S(1)} %bitcast.122), kind=kOutput, calls=%fused_computation.5 | convolution fusion | flops 58200576 | bytes 12805120 | tf_op jit(solution)/shard_map/dot_general | solution.py:32
  217.3 3.6 %fusion.200 = f32[256,6144]{1,0:T(8,128)S(1)} fusion(pred[256,1024]{0,1:T(32,128)(4,1)S(1)} %get-tuple-element.48, bf16[1024,6144]{1,0:T(8,128)(2,1)S(1)} %bitcast.104), kind=kOutput, calls=%fused_computation.298 | convolution fusion | flops 3221225472 | bytes 19136512 | tf_op jit(solution)/shard_map/dot_general | solution.py:32
  221.0 3.6 %convolution_add_fusion.2 = f32[256,6144]{1,0:T(8,128)} fusion(f32[256,6144]{1,0:T(8,128)S(1)} %fusion.200, bf16[18,6144]{1,0:T(8,128)(2,1)S(1)} %copy-done.3, s32[256]{0:T(256)S(1)} %bitcast.121), kind=kOutput, calls=%fused_computation.4 | convolution fusion | flops 58200576 | bytes 12805120 | tf_op jit(solution)/shard_map/dot_general | solution.py:32
  224.6 47.0 %all-gather.6.cloned.1.call-done = bf16[4,512,1536]{2,1,0:T(8,128)(2,1)} async-done(((bf16[4,64,1536]{2,1,0:T(8,128)(2,1)}), bf16[4,512,1536]{2,1,0:T(8,128)(2,1)}) %all-gather.6.cloned.1.call-update) | async-done | bytes 6291472 | tf_op jit(solution)/shard_map/all_gather | solution.py:67
  271.6 2.6 convolution_add_fusion.16
  274.2 2.6 convolution_add_fusion.17
  276.8 2.0 convolution_add_fusion.18
  278.8 2.1 convolution_add_fusion.19
  281.0 2.3 convert_bitcast_fusion.11
  284.0 1.2 copy-done.7
  286.3 1.6 convert_bitcast_fusion.6
  287.9 5.6 %fusion.201 = f32[256,6144]{1,0:T(8,128)} fusion(pred[256,1024]{0,1:T(32,128)(4,1)S(1)} %copy-done.14, bf16[1024,6144]{1,0:T(8,128)(2,1)S(1)} %bitcast.106), kind=kOutput, calls=%fused_computation.299 | convolution fusion | flops 3221225472 | bytes 19136512 | tf_op jit(solution)/shard_map/dot_general | solution.py:32
  293.5 3.8 %convolution_add_fusion.1 = f32[256,6144]{1,0:T(8,128)S(1)} fusion(f32[256,6144]{1,0:T(8,128)} %fusion.201, bf16[18,6144]{1,0:T(8,128)(2,1)S(1)} %copy-done.4, s32[256]{0:T(256)S(1)} %bitcast.120), kind=kOutput, calls=%fused_computation.3 | convolution fusion | flops 58200576 | bytes 12805120 | tf_op jit(solution)/shard_map/dot_general | solution.py:32
  297.3 0.6 convolution_add_fusion.11
  297.9 1.2 convert_bitcast_fusion.3
  299.2 6.5 %fusion.202 = f32[256,6144]{1,0:T(8,128)} fusion(pred[256,1024]{0,1:T(32,128)(4,1)} %get-tuple-element.47, bf16[1024,6144]{1,0:T(8,128)(2,1)S(1)} %bitcast.106), kind=kOutput, calls=%fused_computation.300 | convolution fusion | flops 3221225472 | bytes 19136512 | tf_op jit(solution)/shard_map/dot_general | solution.py:32
  305.7 3.9 %convolution_add_fusion = f32[256,6144]{1,0:T(8,128)S(1)} fusion(f32[256,6144]{1,0:T(8,128)} %fusion.202, bf16[18,6144]{1,0:T(8,128)(2,1)S(1)} %copy-done.4, s32[256]{0:T(256)S(1)} %bitcast.119), kind=kOutput, calls=%fused_computation.2 | convolution fusion | flops 58200576 | bytes 12805120 | tf_op jit(solution)/shard_map/dot_general | solution.py:32
  309.6 0.6 convolution_add_fusion.7
  311.6 0.6 convolution_add_fusion.6
  313.3 0.6 convolution_add_fusion.12
  313.9 0.7 convert_bitcast_fusion.4
  314.6 0.6 convolution_add_fusion.9
  315.5 0.6 convolution_add_fusion.5
  316.5 0.6 convolution_add_fusion.8
  318.9 1.7 maximum_select_fusion
  320.6 5.3 %copy.27 = bf16[256,4,2048]{2,1,0:T(4,128)(2,1)} copy(bf16[256,4,2048]{2,0,1:T(8,128)(2,1)S(1)} %maximum_select_fusion) | data formatting | bytes 8388608
  325.8 5.6 %exponential_reduce_fusion = (f32[256,4,32]{0,2,1:T(8,128)S(1)}, f32[256,4,32]{0,2,1:T(8,128)S(1)}) fusion(s32[256,4,32]{0,2,1:T(8,128)S(1)} %copy-done.22, bf16[32,32,2048,1]{2,1,0,3:T(8,128)(2,1)S(1)} %bitcast.115, bf16[256,4,2048]{2,0,1:T(8,128)(2,1)S(1)} %maximum_select_fusion), kind=kOutput, calls=%fused_computation.9 | convolution fusion | flops 4299096064 | bytes 8781824 | tf_op jit(solution)/shard_map/dot_general | solution.py:90
  331.5 0.7 subtract_select_fusion
  (94 shorter events, 7.9 us)
Async XLA Ops:
  7.2 20.6 %copy-start = (f32[256,2048]{1,0:T(8,128)S(1)}, f32[256,2048]{1,0:T(8,128)}, u32[]{:S(2)}) copy-start(f32[256,2048]{1,0:T(8,128)} %param.10) | copy-start | bytes 6291460
  7.2 76.0 %all-gather.8.cloned.1.call-start = ((), (), s32[]{:S(2)}) async-start(), calls=%async_computation.5 | async-start | bytes 4718592 | tf_op jit(solution)/shard_map/all_gather | solution.py:89
  7.9 198.7 %all-gather.4.cloned.1.call-start = ((), (), s32[]{:S(2)}) async-start(), calls=%async_computation.3 | async-start | bytes 14155776 | tf_op jit(solution)/shard_map/all_gather | solution.py:66
  8.7 262.9 %all-gather.6.cloned.1.call-start = ((), (), s32[]{:S(2)}) async-start(), calls=%async_computation.4 | async-start | bytes 7077888 | tf_op jit(solution)/shard_map/all_gather | solution.py:67
  10.8 14.4 %all-to-all-start = ((s32[32,1,8]{2,1,0:T(1,128)}), s32[32,1,8]{2,1,0:T(1,128)S(1)}, u32[]{:S(2)}, u32[]{:S(2)}) async-start(s32[32,1,8]{2,1,0:T(1,128)} %compare_convert_fusion), calls=%async_computation | async-start | bytes 32768 | tf_op jit(solution)/shard_map/all_to_all | solution.py:76
  25.2 10.2 %all-to-all-start.1 = ((s32[32,1,256]{2,1,0:T(1,128)}), s32[32,1,256]{2,1,0:T(1,128)S(1)}, u32[]{:S(2)}, u32[]{:S(2)}) async-start(s32[32,1,256]{2,1,0:T(1,128)} %reshape.433), calls=%async_computation.1 | async-start | bytes 65536 | tf_op jit(solution)/shard_map/all_to_all | solution.py:75
  30.5 7.8 %copy-start.23 = (s32[256,4]{0,1:T(4,128)S(1)}, s32[256,4]{0,1:T(4,128)}, u32[]{:S(2)}) copy-start(s32[256,4]{0,1:T(4,128)} %param.14) | copy-start | bytes 12292
  30.5 7.8 %copy-start.22 = (s32[256,4,32]{0,2,1:T(8,128)S(1)}, s32[256,4,32]{0,2,1:T(8,128)}, u32[]{:S(2)}) copy-start(s32[256,4,32]{0,2,1:T(8,128)} %param.15) | copy-start | bytes 393220
  35.4 189.2 %all-to-all-start.2 = ((f32[32,8,2048]{2,1,0:T(8,128)}), f32[32,8,2048]{2,1,0:T(8,128)S(1)}, u32[]{:S(2)}, u32[]{:S(2)}) async-start(f32[32,8,2048]{2,1,0:T(8,128)} %bitcast.114), calls=%async_computation.2 | async-start | bytes 4194304 | tf_op jit(solution)/shard_map/all_to_all | solution.py:74
  206.6 7.0 %copy-start.3 = (bf16[18,6144]{1,0:T(8,128)(2,1)S(1)}, bf16[18,6144]{1,0:T(8,128)(2,1)}, u32[]{:S(2)}) copy-start(bf16[18,6144]{1,0:T(8,128)(2,1)} %param.18) | copy-start | bytes 663556
  206.6 10.7 %slice-start = ((s8[12582912]{0:T(1024)(128)(4,1)}), s8[4194304]{0:T(1024)(128)(4,1)S(1)}, s32[]{:S(2)}) async-start(s8[12582912]{0:T(1024)(128)(4,1)} %bitcast.103), calls=%async_computation.6 | async-start | bytes 8388608
  206.6 10.7 %slice-start.1 = ((s8[12582912]{0:T(1024)(128)(4,1)}), s8[4194304]{0:T(1024)(128)(4,1)S(1)}, s32[]{:S(2)}) async-start(s8[12582912]{0:T(1024)(128)(4,1)} %bitcast.103), calls=%async_computation.7 | async-start | bytes 8388608
  213.6 3.7 %slice-start.2 = ((s8[12582912]{0:T(1024)(128)(4,1)}), s8[4194304]{0:T(1024)(128)(4,1)S(1)}, s32[]{:S(2)}) async-start(s8[12582912]{0:T(1024)(128)(4,1)} %bitcast.103), calls=%async_computation.8 | async-start | bytes 8388608
  271.6 5.2 %copy-start.2 = (bf16[4,512,1536]{2,1,0:T(8,128)(2,1)S(1)}, bf16[4,512,1536]{2,1,0:T(8,128)(2,1)}, u32[]{:S(2)}) copy-start(bf16[4,512,1536]{2,1,0:T(8,128)(2,1)} %all-gather.6.cloned.1.call-done) | copy-start | bytes 18874372
  274.2 9.1 %slice-start.6 = ((s8[6291456]{0:T(1024)(128)(4,1)}), s8[4194304]{0:T(1024)(128)(4,1)S(1)}, s32[]{:S(2)}) async-start(s8[6291456]{0:T(1024)(128)(4,1)} %bitcast.107), calls=%async_computation.12 | async-start | bytes 8388608
  278.8 4.5 %slice-start.7 = ((s8[6291456]{0:T(1024)(128)(4,1)}), s8[2097152]{0:T(1024)(128)(4,1)S(1)}, s32[]{:S(2)}) async-start(s8[6291456]{0:T(1024)(128)(4,1)} %bitcast.107), calls=%async_computation.13 | async-start | bytes 4194304
  280.9 6.9 %slice-start.3 = ((s8[12582912]{0:T(1024)(128)(4,1)}), s8[4194304]{0:T(1024)(128)(4,1)S(1)}, s32[]{:S(2)}) async-start(s8[12582912]{0:T(1024)(128)(4,1)} %bitcast.105), calls=%async_computation.9 | async-start | bytes 8388608
  281.0 6.9 %slice-start.4 = ((s8[12582912]{0:T(1024)(128)(4,1)}), s8[4194304]{0:T(1024)(128)(4,1)S(1)}, s32[]{:S(2)}) async-start(s8[12582912]{0:T(1024)(128)(4,1)} %bitcast.105), calls=%async_computation.10 | async-start | bytes 8388608
  283.2 0.8 copy-start.8
  283.2 2.0 copy-start.7
  285.2 1.0 copy-start.9
  285.2 2.6 slice-start.5
  286.3 1.6 copy-start.14
  287.9 5.6 %copy-start.4 = (bf16[18,6144]{1,0:T(8,128)(2,1)S(1)}, bf16[18,6144]{1,0:T(8,128)(2,1)}, u32[]{:S(2)}) copy-start(bf16[18,6144]{1,0:T(8,128)(2,1)} %param.18) | copy-start | bytes 663556
  293.5 3.9 %copy-start.12 = (f32[256,512]{1,0:T(8,128)S(1)}, f32[256,512]{1,0:T(8,128)}, u32[]{:S(2)}) copy-start(f32[256,512]{1,0:T(8,128)} %get-tuple-element.54) | copy-start | bytes 1572868
  305.7 3.9 %copy-start.10 = (f32[256,512]{1,0:T(8,128)S(1)}, f32[256,512]{1,0:T(8,128)}, u32[]{:S(2)}) copy-start(f32[256,512]{1,0:T(8,128)} %get-tuple-element.27) | copy-start | bytes 1572868
  309.6 1.0 copy-start.11
  311.6 1.0 copy-start.5
  312.2 1.1 copy-start.6
  317.5 1.0 copy-start.15
  317.5 1.0 copy-start.16
  317.5 1.1 copy-start.17
  317.5 1.2 copy-start.18
  317.5 1.2 copy-start.19
  317.5 1.3 copy-start.20
  317.5 1.4 copy-start.21
  320.6 5.3 %copy-start.13 = (bf16[1024,2048]{1,0:T(8,128)(2,1)S(1)}, bf16[1024,2048]{1,0:T(8,128)(2,1)}, u32[]{:S(2)}) copy-start(bf16[1024,2048]{1,0:T(8,128)(2,1)} %copy.26) | copy-start | bytes 12582916
  325.8 6.3 %copy-start.1 = (f32[256,2048]{1,0:T(8,128)S(1)}, f32[256,2048]{1,0:T(8,128)}, u32[]{:S(2)}) copy-start(f32[256,2048]{1,0:T(8,128)} %param.10) | copy-start | bytes 6291460
Sparse Core Ops, SparseCore 0:
  9.6 73.5 all-gather.7
  84.8 121.7 all-gather.3
  208.2 63.3 all-gather.5
where the time goes:
time: 339 us
  waiting for transfers between devices  217 us (64%)
  matrix products  59.7 us (18%)
  local copies, waits for them, and re-layouts  20.3 us (6%)
  other arithmetic  15 us (4%)
  between operations  14.3 us (4%)
  starting transfers between devices  12.7 us (4%)
    all_gather x1, waiting for transfers between devices, on_device(): stoch_full = lax.all_gather(w_stoch, 'gy', axis=0, tiled=True)  117 us
    all_gather x1, waiting for transfers between devices, on_device(): deter_full = lax.all_gather(w_deter, 'gy', axis=1, tiled=True)  47 us
    all_gather x1, waiting for transfers between devices, on_device(): prior_full = lax.all_gather(w_prior, 'gy', axis=0, tiled=True)  41.9 us
    dot_general x4, matrix products, imagine(): jnp.dot(onehot, stoch_full, preferred_element_type=jnp.float32)  22.7 us
    dot_general x16, matrix products, imagine(): jnp.dot(before.astype(jnp.bfloat16), deter_full[b], preferred_element_typ...  16.3 us
    dot_general x4, matrix products, imagine(): jnp.dot(act_hot, act_table, preferred_element_type=jnp.float32)  15 us
    unnamed x68, local copies, waits for them, and re-layouts  9.44 us
    concatenate x11, other arithmetic, imagine(): states.append(jnp.concatenate(pieces, 1).astype(jnp.bfloat16))  8.3 us
  transfers between devices with their start and end apart: 6, of which 5 were waited for; matrix products, arithmetic and copies ran while one was open for 10% of the time, Pallas kernels for 0%

commit v1 on v0

--- a/solution.py
+++ b/solution.py
@@ -86,7 +86,24 @@
         act_table,
     )
     states = jnp.where(live[:, None, None] > 0, states, jnp.zeros_like(states))
-    prior_full = lax.all_gather(w_prior, "gy", axis=0, tiled=True)
+    size, index, rows_2 = (lax.axis_size("gy"), lax.axis_index("gy"), w_prior.shape[0])
+    right = [(i, (i + 1) % size) for i in range(size)]
+    behind = [(i, (i - 1) % size) for i in range(size)]
+    filled = jnp.zeros((*w_prior.shape[:0], size * rows_2, *w_prior.shape[0 + 1 :]), w_prior.dtype)
+    filled = lax.dynamic_update_slice_in_dim(filled, w_prior, index * rows_2, axis=0)
+    from_left = from_right = w_prior
+    half = size // 2
+    for step_2 in range(1, half + 1):
+        from_left = lax.ppermute(from_left, "gy", right)
+        filled = lax.dynamic_update_slice_in_dim(
+            filled, from_left, (index - step_2) % size * rows_2, axis=0
+        )
+        if step_2 < size - half:
+            from_right = lax.ppermute(from_right, "gy", behind)
+            filled = lax.dynamic_update_slice_in_dim(
+                filled, from_right, (index + step_2) % size * rows_2, axis=0
+            )
+    prior_full = filled
     logits = jnp.dot(
         states.reshape(slots * STEPS, deter), prior_full, preferred_element_type=jnp.float32
     )

time: 339 us -> 349 us (1.029); the launches traced: 339 us -> 343 us
  waiting for transfers between devices: 217 us -> 145 us
  starting transfers between devices: 12.7 us -> 60.2 us
  matrix products: 59.7 us -> 75.2 us
  local copies, waits for them, and re-layouts: 20.3 us -> 33 us
    all_gather x1, waiting for transfers between devices: 117 us -> 1.18 us  [on_device(): stoch_full = lax.all_gather(w_stoch, 'gy', axis=0, tiled=True)]
    ppermute x0 -> x7, waiting for transfers between devices: none -> 86.3 us  [the longest x3 67.6 us: on_device(): from_right = lax.ppermute(from_right, 'gy', behind)]
    all_gather x1 -> x0, waiting for transfers between devices: 41.9 us -> none  [on_device(): prior_full = lax.all_gather(w_prior, 'gy', axis=0, tiled=True)]
    all_to_all x1, starting transfers between devices: 2.57 us -> 22.8 us  [on_device(): lax.all_to_all(first, ('gx', 'gy'), split_axis=0, concat_axis=0, tiled=True)]
    all_to_all x1, starting transfers between devices: 2.73 us -> 21.1 us  [on_device(): lax.all_to_all(start, ('gx', 'gy'), split_axis=0, concat_axis=0, tiled=True)]
    dot_general x4, matrix products: 22.7 us -> 34.9 us  [imagine(): jnp.dot(onehot, stoch_full, preferred_element_type=jnp.float32)]
    ppermute x0 -> x7, starting transfers between devices: none -> 11.7 us  [the longest x3 11.2 us: on_device(): from_right = lax.ppermute(from_right, 'gy', behind)]
    ppermute x0 -> x7, local copies, waits for them, and re-layouts: none -> 8.71 us  [the longest x4 4.98 us: on_device(): from_left = lax.ppermute(from_left, 'gy', right)]
  transfers between devices with their start and end apart: 6 -> 12, of which waited for: 5 -> 7; matrix products, arithmetic and copies ran while one was open for 10% -> 14% of each run, Pallas kernels for 0% -> 0%
where the time goes in v1:
time: 349 us; the launch traced here: 343 us
  waiting for transfers between devices  145 us (42%)
  matrix products  75.2 us (22%)
  starting transfers between devices  60.2 us (17%)
  local copies, waits for them, and re-layouts  33 us (9%)
  between operations  14.9 us (4%)
  other arithmetic  14.8 us (4%)
    ppermute x3, waiting for transfers between devices, on_device(): from_right = lax.ppermute(from_right, 'gy', behind)  67.6 us
    all_gather x1, waiting for transfers between devices, on_device(): deter_full = lax.all_gather(w_deter, 'gy', axis=1, tiled=True)  48.1 us
    dot_general x4, matrix products, imagine(): jnp.dot(onehot, stoch_full, preferred_element_type=jnp.float32)  34.9 us
    all_to_all x1, starting transfers between devices, on_device(): lax.all_to_all(first, ('gx', 'gy'), split_axis=0, concat_axis=0, tiled=True)  22.8 us
    all_to_all x1, starting transfers between devices, on_device(): lax.all_to_all(start, ('gx', 'gy'), split_axis=0, concat_axis=0, tiled=True)  21.1 us
    ppermute x4, waiting for transfers between devices, on_device(): from_left = lax.ppermute(from_left, 'gy', right)  18.7 us
    dot_general x16, matrix products, imagine(): jnp.dot(before.astype(jnp.bfloat16), deter_full[b], preferred_element_typ...  16.3 us
    dot_general x4, matrix products, imagine(): jnp.dot(act_hot, act_table, preferred_element_type=jnp.float32)  15.6 us
  transfers between devices with their start and end apart: 12, of which 7 were waited for; matrix products, arithmetic and copies ran while one was open for 14% of the time, Pallas kernels for 0%

profile of v1, /device:TPU:0, one launch (start us, length us, event | category | flops | bytes accessed | tf_op | source)
XLA Modules:
  0.0 343.0 jit_solution(3446384621733141348)
XLA Ops:
  9.2 4.1 %collective-permute-start.1 = (bf16[256,1024]{1,0:T(8,128)(2,1)}, bf16[256,1024]{1,0:T(8,128)(2,1)}, u32[]{:S(2)}, u32[]{:S(2)}) collective-permute-start(bf16[256,1024]{1,0:T(8,128)(2,1)} %param.19), channel_id=1, source_target_pairs={{0,7},{1,0},{2,1},{3,2},{4,3},{5,4},{6,5},{7,6},{8,15},{9,8},{10,9... | collective-permute-start | bytes 1572872 | tf_op jit(solution)/shard_map/ppermute | solution.py:102
  13.3 1.4 compare_convert_fusion
  14.7 4.5 %all-to-all-start = ((s32[32,1,8]{2,1,0:T(1,128)}), s32[32,1,8]{2,1,0:T(1,128)S(1)}, u32[]{:S(2)}, u32[]{:S(2)}) async-start(s32[32,1,8]{2,1,0:T(1,128)} %compare_convert_fusion), calls=%async_computation | async-start | bytes 32768 | tf_op jit(solution)/shard_map/all_to_all | solution.py:76
  19.2 4.3 %collective-permute-done = bf16[256,1024]{1,0:T(8,128)(2,1)} collective-permute-done((bf16[256,1024]{1,0:T(8,128)(2,1)}, bf16[256,1024]{1,0:T(8,128)(2,1)}, u32[]{:S(2)}, u32[]{:S(2)}) %collective-permute-start) | collective-permute-done | bytes 524320 | tf_op jit(solution)/shard_map/ppermute | solution.py:97
  24.3 4.7 %collective-permute-done.1 = bf16[256,1024]{1,0:T(8,128)(2,1)} collective-permute-done((bf16[256,1024]{1,0:T(8,128)(2,1)}, bf16[256,1024]{1,0:T(8,128)(2,1)}, u32[]{:S(2)}, u32[]{:S(2)}) %collective-permute-start.1) | collective-permute-done | bytes 524320 | tf_op jit(solution)/shard_map/ppermute | solution.py:102
  29.0 3.7 %collective-permute-start.3 = (bf16[256,1024]{1,0:T(8,128)(2,1)}, bf16[256,1024]{1,0:T(8,128)(2,1)}, u32[]{:S(2)}, u32[]{:S(2)}) collective-permute-start(bf16[256,1024]{1,0:T(8,128)(2,1)} %collective-permute-done.1), channel_id=1, source_target_pairs={{0,7},{1,0},{2,1},{3,2},{4,3},{5,4},{6,5},{7,6},{8,15},{9,8},{10,9... | collective-permute-start | bytes 1572872 | tf_op jit(solution)/shard_map/ppermute | solution.py:102
  35.9 14.4 %collective-permute-done.2 = bf16[256,1024]{1,0:T(8,128)(2,1)} collective-permute-done((bf16[256,1024]{1,0:T(8,128)(2,1)}, bf16[256,1024]{1,0:T(8,128)(2,1)}, u32[]{:S(2)}, u32[]{:S(2)}) %collective-permute-start.2) | collective-permute-done | bytes 524320 | tf_op jit(solution)/shard_map/ppermute | solution.py:97
  50.4 22.8 %all-to-all-start.1 = ((s32[32,1,256]{2,1,0:T(1,128)}), s32[32,1,256]{2,1,0:T(1,128)S(1)}, u32[]{:S(2)}, u32[]{:S(2)}) async-start(s32[32,1,256]{2,1,0:T(1,128)} %reshape.433), calls=%async_computation.1 | async-start | bytes 65536 | tf_op jit(solution)/shard_map/all_to_all | solution.py:75
  73.4 2.7 gather_fusion.1
  76.1 7.9 %all-to-all-done.1 = s32[32,1,256]{2,1,0:T(1,128)S(1)} async-done(((s32[32,1,256]{2,1,0:T(1,128)}), s32[32,1,256]{2,1,0:T(1,128)S(1)}, u32[]{:S(2)}, u32[]{:S(2)}) %all-to-all-start.1) | async-done | bytes 32800 | tf_op jit(solution)/shard_map/all_to_all | solution.py:75
  84.0 21.1 %all-to-all-start.2 = ((f32[32,8,2048]{2,1,0:T(8,128)}), f32[32,8,2048]{2,1,0:T(8,128)S(1)}, u32[]{:S(2)}, u32[]{:S(2)}) async-start(f32[32,8,2048]{2,1,0:T(8,128)} %bitcast.115), calls=%async_computation.2 | async-start | bytes 4194304 | tf_op jit(solution)/shard_map/all_to_all | solution.py:74
  105.1 2.5 broadcast_in_dim.47
  107.6 0.9 constant_dynamic-update-slice_fusion.7
  108.6 3.4 collective-permute-start.5
  113.5 1.5 bitcast_compare_fusion
  115.1 1.2 copy.41
  116.3 1.2 copy.42
  117.6 0.9 constant_dynamic-update-slice_fusion.6
  119.3 1.2 copy.43
  120.6 1.2 copy.44
  123.5 1.2 copy.45
  124.8 62.9 %collective-permute-done.5 = bf16[256,1024]{1,0:T(8,128)(2,1)} collective-permute-done((bf16[256,1024]{1,0:T(8,128)(2,1)}, bf16[256,1024]{1,0:T(8,128)(2,1)}, u32[]{:S(2)}, u32[]{:S(2)}) %collective-permute-start.5) | collective-permute-done | bytes 524320 | tf_op jit(solution)/shard_map/ppermute | solution.py:102
  187.7 1.2 copy.46
  188.9 0.9 constant_dynamic-update-slice_fusion.2
  189.8 0.9 constant_dynamic-update-slice_fusion.1
  190.7 1.2 copy.47
  192.0 0.9 constant_dynamic-update-slice_fusion
  192.9 1.2 all-gather.3.cloned.1.call-done
  194.0 7.2 %fusion.199 = f32[256,6144]{1,0:T(8,128)S(1)} fusion(pred[256,1024]{0,1:T(32,128)(4,1)} %get-tuple-element.50, bf16[1024,6144]{1,0:T(8,128)(2,1)} %all-gather.3.cloned.1.call-done), kind=kOutput, calls=%fused_computation.305 | convolution fusion | flops 3221225472 | bytes 19136512 | tf_op jit(solution)/shard_map/dot_general | solution.py:32
  201.3 4.2 %convolution_add_fusion.3 = f32[256,6144]{1,0:T(8,128)} fusion(f32[256,6144]{1,0:T(8,128)S(1)} %fusion.199, bf16[18,6144]{1,0:T(8,128)(2,1)S(1)} %copy-done.3, s32[256]{0:T(256)S(1)} %bitcast.121), kind=kOutput, calls=%fused_computation.5 | convolution fusion | flops 58200576 | bytes 12805120 | tf_op jit(solution)/shard_map/dot_general | solution.py:32
  205.4 3.6 %fusion.200 = f32[256,6144]{1,0:T(8,128)S(1)} fusion(pred[256,1024]{0,1:T(32,128)(4,1)S(1)} %get-tuple-element.48, bf16[1024,6144]{1,0:T(8,128)(2,1)S(1)} %bitcast.105), kind=kOutput, calls=%fused_computation.306 | convolution fusion | flops 3221225472 | bytes 19136512 | tf_op jit(solution)/shard_map/dot_general | solution.py:32
  209.1 3.7 %convolution_add_fusion.2 = f32[256,6144]{1,0:T(8,128)} fusion(f32[256,6144]{1,0:T(8,128)S(1)} %fusion.200, bf16[18,6144]{1,0:T(8,128)(2,1)S(1)} %copy-done.3, s32[256]{0:T(256)S(1)} %bitcast.120), kind=kOutput, calls=%fused_computation.4 | convolution fusion | flops 58200576 | bytes 12805120 | tf_op jit(solution)/shard_map/dot_general | solution.py:32
  212.8 48.1 %all-gather.5.cloned.1.call-done = bf16[4,512,1536]{2,1,0:T(8,128)(2,1)} async-done(((bf16[4,64,1536]{2,1,0:T(8,128)(2,1)}), bf16[4,512,1536]{2,1,0:T(8,128)(2,1)}) %all-gather.5.cloned.1.call-update) | async-done | bytes 6291472 | tf_op jit(solution)/shard_map/all_gather | solution.py:67
  260.9 2.6 convolution_add_fusion.16
  263.5 2.6 convolution_add_fusion.17
  266.1 2.0 convolution_add_fusion.18
  268.1 2.1 convolution_add_fusion.19
  270.3 2.3 convert_bitcast_fusion.11
  273.4 1.2 copy-done.7
  275.6 1.6 convert_bitcast_fusion.6
  277.2 17.5 %fusion.201 = f32[256,6144]{1,0:T(8,128)} fusion(pred[256,1024]{0,1:T(32,128)(4,1)S(1)} %copy-done.13, bf16[1024,6144]{1,0:T(8,128)(2,1)S(1)} %bitcast.107), kind=kOutput, calls=%fused_computation.307 | convolution fusion | flops 3221225472 | bytes 19136512 | tf_op jit(solution)/shard_map/dot_general | solution.py:32
  294.7 3.8 %convolution_add_fusion.1 = f32[256,6144]{1,0:T(8,128)S(1)} fusion(f32[256,6144]{1,0:T(8,128)} %fusion.201, bf16[18,6144]{1,0:T(8,128)(2,1)S(1)} %copy-done.4, s32[256]{0:T(256)S(1)} %bitcast.119), kind=kOutput, calls=%fused_computation.3 | convolution fusion | flops 58200576 | bytes 12805120 | tf_op jit(solution)/shard_map/dot_general | solution.py:32
  299.1 1.3 convert_bitcast_fusion.3
  300.4 6.6 %fusion.202 = f32[256,6144]{1,0:T(8,128)} fusion(pred[256,1024]{0,1:T(32,128)(4,1)} %get-tuple-element.47, bf16[1024,6144]{1,0:T(8,128)(2,1)S(1)} %bitcast.107), kind=kOutput, calls=%fused_computation.308 | convolution fusion | flops 3221225472 | bytes 19136512 | tf_op jit(solution)/shard_map/dot_general | solution.py:32
  307.0 3.9 %convolution_add_fusion = f32[256,6144]{1,0:T(8,128)S(1)} fusion(f32[256,6144]{1,0:T(8,128)} %fusion.202, bf16[18,6144]{1,0:T(8,128)(2,1)S(1)} %copy-done.4, s32[256]{0:T(256)S(1)} %bitcast.118), kind=kOutput, calls=%fused_computation.2 | convolution fusion | flops 58200576 | bytes 12805120 | tf_op jit(solution)/shard_map/dot_general | solution.py:32
  320.2 1.4 maximum_select_fusion
  321.6 5.3 %copy.48 = bf16[256,4,2048]{2,1,0:T(4,128)(2,1)} copy(bf16[256,4,2048]{2,0,1:T(8,128)(2,1)S(1)} %maximum_select_fusion) | data formatting | bytes 8388608
  326.9 8.3 %exponential_reduce_fusion = (f32[256,4,32]{0,2,1:T(8,128)S(1)}, f32[256,4,32]{0,2,1:T(8,128)S(1)}) fusion(s32[256,4,32]{0,2,1:T(8,128)S(1)} %copy-done.22, bf16[32,32,2048,1]{2,1,0,3:T(8,128)(2,1)} %bitcast.40, bf16[256,4,2048]{2,0,1:T(8,128)(2,1)S(1)} %maximum_select_fusion), kind=kOutput, calls=%fused_computation.9 | convolution fusion | flops 4299096064 | bytes 8781824 | tf_op jit(solution)/shard_map/dot_general | solution.py:107
  (121 shorter events, 22.7 us)
Async XLA Ops:
  7.2 66.3 %copy-start = (f32[256,2048]{1,0:T(8,128)S(1)}, f32[256,2048]{1,0:T(8,128)}, u32[]{:S(2)}) copy-start(f32[256,2048]{1,0:T(8,128)} %param.10) | copy-start | bytes 6291460
  7.2 66.0 %copy-start.21 = (bf16[256,1024]{1,0:T(8,128)(2,1)S(1)}, bf16[256,1024]{1,0:T(8,128)(2,1)}, u32[]{:S(2)}) copy-start(bf16[256,1024]{1,0:T(8,128)(2,1)} %param.19) | copy-start | bytes 1572868
  7.2 66.0 %copy-start.23 = (s32[256,4]{0,1:T(4,128)S(1)}, s32[256,4]{0,1:T(4,128)}, u32[]{:S(2)}) copy-start(s32[256,4]{0,1:T(4,128)} %param.14) | copy-start | bytes 12292
  7.2 186.8 %all-gather.3.cloned.1.call-start = ((), (), s32[]{:S(2)}) async-start(), calls=%async_computation.3 | async-start | bytes 14155776 | tf_op jit(solution)/shard_map/all_gather | solution.py:66
  7.9 253.0 %all-gather.5.cloned.1.call-start = ((), (), s32[]{:S(2)}) async-start(), calls=%async_computation.4 | async-start | bytes 7077888 | tf_op jit(solution)/shard_map/all_gather | solution.py:67
  8.7 14.8 %collective-permute-start = (bf16[256,1024]{1,0:T(8,128)(2,1)}, bf16[256,1024]{1,0:T(8,128)(2,1)}, u32[]{:S(2)}, u32[]{:S(2)}) collective-permute-start(bf16[256,1024]{1,0:T(8,128)(2,1)} %param.19), channel_id=1, source_target_pairs={{0,1},{1,2},{2,3},{3,4},{4,5},{5,6},{6,7},{7,0},{8,9},{9,10},{10,1... | collective-permute-start | bytes 1572872 | tf_op jit(solution)/shard_map/ppermute | solution.py:97
  9.2 19.8 %collective-permute-start.1 = (bf16[256,1024]{1,0:T(8,128)(2,1)}, bf16[256,1024]{1,0:T(8,128)(2,1)}, u32[]{:S(2)}, u32[]{:S(2)}) collective-permute-start(bf16[256,1024]{1,0:T(8,128)(2,1)} %param.19), channel_id=1, source_target_pairs={{0,7},{1,0},{2,1},{3,2},{4,3},{5,4},{6,5},{7,6},{8,15},{9,8},{10,9... | collective-permute-start | bytes 1572872 | tf_op jit(solution)/shard_map/ppermute | solution.py:102
  14.7 35.7 %all-to-all-start = ((s32[32,1,8]{2,1,0:T(1,128)}), s32[32,1,8]{2,1,0:T(1,128)S(1)}, u32[]{:S(2)}, u32[]{:S(2)}) async-start(s32[32,1,8]{2,1,0:T(1,128)} %compare_convert_fusion), calls=%async_computation | async-start | bytes 32768 | tf_op jit(solution)/shard_map/all_to_all | solution.py:76
  23.5 26.9 %collective-permute-start.2 = (bf16[256,1024]{1,0:T(8,128)(2,1)}, bf16[256,1024]{1,0:T(8,128)(2,1)}, u32[]{:S(2)}, u32[]{:S(2)}) collective-permute-start(bf16[256,1024]{1,0:T(8,128)(2,1)} %collective-permute-done), channel_id=1, source_target_pairs={{0,1},{1,2},{2,3},{3,4},{4,5},{5,6},{6,7},{7,0},{8,9},{9,10},{10,1... | collective-permute-start | bytes 1572872 | tf_op jit(solution)/shard_map/ppermute | solution.py:97
  29.0 79.6 %collective-permute-start.3 = (bf16[256,1024]{1,0:T(8,128)(2,1)}, bf16[256,1024]{1,0:T(8,128)(2,1)}, u32[]{:S(2)}, u32[]{:S(2)}) collective-permute-start(bf16[256,1024]{1,0:T(8,128)(2,1)} %collective-permute-done.1), channel_id=1, source_target_pairs={{0,7},{1,0},{2,1},{3,2},{4,3},{5,4},{6,5},{7,6},{8,15},{9,8},{10,9... | collective-permute-start | bytes 1572872 | tf_op jit(solution)/shard_map/ppermute | solution.py:102
  50.3 68.1 %collective-permute-start.4 = (bf16[256,1024]{1,0:T(8,128)(2,1)}, bf16[256,1024]{1,0:T(8,128)(2,1)}, u32[]{:S(2)}, u32[]{:S(2)}) collective-permute-start(bf16[256,1024]{1,0:T(8,128)(2,1)} %collective-permute-done.2), channel_id=1, source_target_pairs={{0,1},{1,2},{2,3},{3,4},{4,5},{5,6},{6,7},{7,0},{8,9},{9,10},{10,1... | collective-permute-start | bytes 1572872 | tf_op jit(solution)/shard_map/ppermute | solution.py:97
  50.4 33.7 %all-to-all-start.1 = ((s32[32,1,256]{2,1,0:T(1,128)}), s32[32,1,256]{2,1,0:T(1,128)S(1)}, u32[]{:S(2)}, u32[]{:S(2)}) async-start(s32[32,1,256]{2,1,0:T(1,128)} %reshape.433), calls=%async_computation.1 | async-start | bytes 65536 | tf_op jit(solution)/shard_map/all_to_all | solution.py:75
  84.0 128.8 %all-to-all-start.2 = ((f32[32,8,2048]{2,1,0:T(8,128)}), f32[32,8,2048]{2,1,0:T(8,128)S(1)}, u32[]{:S(2)}, u32[]{:S(2)}) async-start(f32[32,8,2048]{2,1,0:T(8,128)} %bitcast.115), calls=%async_computation.2 | async-start | bytes 4194304 | tf_op jit(solution)/shard_map/all_to_all | solution.py:74
  108.6 79.1 %collective-permute-start.5 = (bf16[256,1024]{1,0:T(8,128)(2,1)}, bf16[256,1024]{1,0:T(8,128)(2,1)}, u32[]{:S(2)}, u32[]{:S(2)}) collective-permute-start(bf16[256,1024]{1,0:T(8,128)(2,1)} %collective-permute-done.3), channel_id=1, source_target_pairs={{0,7},{1,0},{2,1},{3,2},{4,3},{5,4},{6,5},{7,6},{8,15},{9,8},{10,9... | collective-permute-start | bytes 1572872 | tf_op jit(solution)/shard_map/ppermute | solution.py:102
  118.5 72.3 %collective-permute-start.6 = (bf16[256,1024]{1,0:T(8,128)(2,1)}, bf16[256,1024]{1,0:T(8,128)(2,1)}, u32[]{:S(2)}, u32[]{:S(2)}) collective-permute-start(bf16[256,1024]{1,0:T(8,128)(2,1)} %collective-permute-done.4), channel_id=1, source_target_pairs={{0,1},{1,2},{2,3},{3,4},{4,5},{5,6},{6,7},{7,0},{8,9},{9,10},{10,1... | collective-permute-start | bytes 1572872 | tf_op jit(solution)/shard_map/ppermute | solution.py:97
  194.0 7.2 %copy-start.3 = (bf16[18,6144]{1,0:T(8,128)(2,1)S(1)}, bf16[18,6144]{1,0:T(8,128)(2,1)}, u32[]{:S(2)}) copy-start(bf16[18,6144]{1,0:T(8,128)(2,1)} %param.18) | copy-start | bytes 663556
  194.0 11.4 %slice-start = ((s8[12582912]{0:T(1024)(128)(4,1)}), s8[4194304]{0:T(1024)(128)(4,1)S(1)}, s32[]{:S(2)}) async-start(s8[12582912]{0:T(1024)(128)(4,1)} %bitcast.104), calls=%async_computation.5 | async-start | bytes 8388608
  194.0 11.4 %slice-start.1 = ((s8[12582912]{0:T(1024)(128)(4,1)}), s8[4194304]{0:T(1024)(128)(4,1)S(1)}, s32[]{:S(2)}) async-start(s8[12582912]{0:T(1024)(128)(4,1)} %bitcast.104), calls=%async_computation.6 | async-start | bytes 8388608
  201.2 4.2 %slice-start.2 = ((s8[12582912]{0:T(1024)(128)(4,1)}), s8[4194304]{0:T(1024)(128)(4,1)S(1)}, s32[]{:S(2)}) async-start(s8[12582912]{0:T(1024)(128)(4,1)} %bitcast.104), calls=%async_computation.7 | async-start | bytes 8388608
  260.9 5.2 %copy-start.2 = (bf16[4,512,1536]{2,1,0:T(8,128)(2,1)S(1)}, bf16[4,512,1536]{2,1,0:T(8,128)(2,1)}, u32[]{:S(2)}) copy-start(bf16[4,512,1536]{2,1,0:T(8,128)(2,1)} %all-gather.5.cloned.1.call-done) | copy-start | bytes 18874372
  263.5 9.1 %slice-start.6 = ((s8[6291456]{0:T(1024)(128)(4,1)}), s8[4194304]{0:T(1024)(128)(4,1)S(1)}, s32[]{:S(2)}) async-start(s8[6291456]{0:T(1024)(128)(4,1)} %bitcast.108), calls=%async_computation.11 | async-start | bytes 8388608
  268.1 4.4 %slice-start.7 = ((s8[6291456]{0:T(1024)(128)(4,1)}), s8[2097152]{0:T(1024)(128)(4,1)S(1)}, s32[]{:S(2)}) async-start(s8[6291456]{0:T(1024)(128)(4,1)} %bitcast.108), calls=%async_computation.12 | async-start | bytes 4194304
  270.3 6.9 %slice-start.3 = ((s8[12582912]{0:T(1024)(128)(4,1)}), s8[4194304]{0:T(1024)(128)(4,1)S(1)}, s32[]{:S(2)}) async-start(s8[12582912]{0:T(1024)(128)(4,1)} %bitcast.106), calls=%async_computation.8 | async-start | bytes 8388608
  270.3 6.9 %slice-start.4 = ((s8[12582912]{0:T(1024)(128)(4,1)}), s8[4194304]{0:T(1024)(128)(4,1)S(1)}, s32[]{:S(2)}) async-start(s8[12582912]{0:T(1024)(128)(4,1)} %bitcast.106), calls=%async_computation.9 | async-start | bytes 8388608
  272.6 0.8 copy-start.8
  272.6 2.0 copy-start.7
  274.5 1.0 copy-start.9
  274.5 2.6 slice-start.5
  275.6 1.6 copy-start.13
  277.2 17.5 %copy-start.4 = (bf16[18,6144]{1,0:T(8,128)(2,1)S(1)}, bf16[18,6144]{1,0:T(8,128)(2,1)}, u32[]{:S(2)}) copy-start(bf16[18,6144]{1,0:T(8,128)(2,1)} %param.18) | copy-start | bytes 663556
  294.7 3.9 %copy-start.12 = (f32[256,512]{1,0:T(8,128)S(1)}, f32[256,512]{1,0:T(8,128)}, u32[]{:S(2)}) copy-start(f32[256,512]{1,0:T(8,128)} %get-tuple-element.54) | copy-start | bytes 1572868
  307.0 3.9 %copy-start.10 = (f32[256,512]{1,0:T(8,128)S(1)}, f32[256,512]{1,0:T(8,128)}, u32[]{:S(2)}) copy-start(f32[256,512]{1,0:T(8,128)} %get-tuple-element.27) | copy-start | bytes 1572868
  310.9 1.0 copy-start.11
  312.9 1.0 copy-start.5
  313.5 1.1 copy-start.6
  318.8 1.0 copy-start.14
  318.8 1.0 copy-start.15
  318.8 1.1 copy-start.16
  318.8 1.2 copy-start.17
  318.8 1.2 copy-start.18
  318.8 1.3 copy-start.19
  318.8 1.4 copy-start.20
  321.6 5.3 %copy-start.22 = (s32[256,4,32]{0,2,1:T(8,128)S(1)}, s32[256,4,32]{0,2,1:T(8,128)}, u32[]{:S(2)}) copy-start(s32[256,4,32]{0,2,1:T(8,128)} %param.15) | copy-start | bytes 393220
  326.9 9.0 %copy-start.1 = (f32[256,2048]{1,0:T(8,128)S(1)}, f32[256,2048]{1,0:T(8,128)}, u32[]{:S(2)}) copy-start(f32[256,2048]{1,0:T(8,128)} %param.10) | copy-start | bytes 6291460
Sparse Core Ops, SparseCore 0:
  9.7 184.3 all-gather.2
  195.6 65.2 all-gather.4
